TPU v7x, 16 devices: a whole 2x2x2 slice. The times are simulated.
16 devices in a mesh: right: 4 (over z, y), left: 4 (over x, core).
Axes of the slice: x: 2, y: 2, z: 2, core: 2. Of those that a mesh axis runs over, the one named last changes fastest.
Arguments:
- psi_init: float32 [1536, 3, 3, 1536], P('left', None, None, 'right')
- env_left: float32 [1536, 5, 1536], P('left')
- env_right: float32 [1536, 5, 1536], P('right')
- mpo_pair: float32 [5, 5, 3, 3, 3, 3], replicated
Outputs:
- output 1: float32 [5], replicated
- output 2: float32 [5], replicated
- output 3: float32 [1536, 3, 3, 1536], P('left', None, None, 'right')
All inputs are finite; a program needn't handle non-finite values.
Results may differ from a plain program's by a relative error of at most 0.001.
Values sent between devices are 32-bit elements.
A program may use at most 1 GiB of HBM per device.

v0:
```python
import math
import jax
import jax.numpy as jnp
from jax import lax
from jax.sharding import PartitionSpec as P

KRYLOV_STEPS = 5
PREC_MODE = lax.Precision.HIGHEST
BOTH_AXES = ("right", "left")


def project_out(krylov_basis, residual, coeffs):
    for vec_idx, basis_vec in enumerate(krylov_basis):
        residual = residual - coeffs[vec_idx] * basis_vec
    return residual


def global_dots(krylov_basis, residual):
    local_dots = jnp.stack([jnp.sum(basis_vec * residual) for basis_vec in krylov_basis])
    return lax.psum(local_dots, BOTH_AXES)


def solution(mesh):
    n_devices = mesh.shape["left"] * mesh.shape["right"]
    psi_spec = P("left", None, None, "right")

    def local_fn(psi_loc, env_left, env_right, mpo_pair):
        left_full = lax.all_to_all(env_left, "left", 2, 0, tiled=True)

        def apply_ham(in_vec):
            vec_full = lax.all_gather(in_vec, "left", axis=0, tiled=True)
            stage_one = jnp.einsum("alc,asub->lcsub", left_full, vec_full, precision=PREC_MODE, preferred_element_type=jnp.float32)
            stage_two = jnp.einsum("lrsutv,lcsub->rtvcb", mpo_pair, stage_one, precision=PREC_MODE, preferred_element_type=jnp.float32)
            part_out = jnp.einsum("rtvcb,bre->tvce", stage_two, env_right, precision=PREC_MODE, preferred_element_type=jnp.float32)
            reduced = lax.psum_scatter(part_out, "right", scatter_dimension=3, tiled=True)
            return jnp.transpose(reduced, (2, 0, 1, 3))

        init_norm = jnp.sqrt(lax.psum(jnp.sum(psi_loc * psi_loc), BOTH_AXES))
        krylov_basis = [psi_loc / init_norm]
        alpha_list = []
        beta_list = []
        for step_idx in range(KRYLOV_STEPS):
            residual = apply_ham(krylov_basis[-1])
            first_pass = global_dots(krylov_basis, residual)
            alpha_list.append(first_pass[-1])
            residual = project_out(krylov_basis, residual, first_pass)
            second_pass = global_dots(krylov_basis, residual)
            residual = project_out(krylov_basis, residual, second_pass)
            beta_val = jnp.sqrt(lax.psum(jnp.sum(residual * residual), BOTH_AXES))
            beta_list.append(beta_val)
            krylov_basis.append(residual / beta_val)
        out_scale = math.sqrt(float(psi_loc.size * n_devices))
        return jnp.stack(alpha_list), jnp.stack(beta_list), krylov_basis[-1] * out_scale

    lanczos_run = jax.shard_map(
        local_fn,
        mesh=mesh,
        in_specs=(psi_spec, P("left", None, None), P("right", None, None), P()),
        out_specs=(P(), P(), psi_spec),
        check_vma=False,
    )
    return lanczos_run
```

profile of v0, /device:TPU:0, one launch (start us, length us, event | category | flops | bytes accessed | tf_op | source)
XLA Modules:
  0.0 4559.7 jit_solution(11313862422435896236)
XLA Ops:
  84.2 308.7 %all-to-all-done = f32[384,5,1536]{0,1,2:T(8,128)} async-done(((f32[384,5,1536]{0,1,2:T(8,128)}), f32[384,5,1536]{0,1,2:T(8,128)}, u32[]{:S(2)}, u32[]{:S(2)}) %all-to-all-start) | async-done | bytes 11796512 | tf_op jit(solution)/shard_map/all_to_all | solution.py:28
  408.6 150.4 %fusion.65 = f32[5,384,3,3,384,1,1]{1,4,0,3,2,6,5:T(8,128)} fusion(f32[1536,5,384,1,1]{2,0,1,4,3:T(8,128)} %bitcast.292, f32[1536,3,3,384]{0,3,2,1:T(8,128)} %all-gather.6.cloned.1.call-done), kind=kOutput, calls=%fused_computation.45 | convolution fusion | flops 122305904640 | bytes 59572224 | tf_op jit(solution)/shard_map/alc,asub->lcsub/dot_general | solution.py:32
  634.6 164.9 %fusion.45 = f32[3,3,384,1536]{2,3,1,0:T(8,128)} fusion(f32[5,3,3,384,384]{3,0,2,1,4:T(8,128)} %fusion.30, f32[384,5,1536]{2,0,1:T(8,128)} %param.6), kind=kOutput, calls=%fused_computation.35 | convolution fusion | flops 122305904640 | bytes 59572224 | tf_op jit(solution)/shard_map/rtvcb,bre->tvce/dot_general | solution.py:34
  799.5 186.0 %reduce-scatter.6.cloned.1.call-done = f32[3,3,384,384]{2,3,1,0:T(8,128)} async-done(((f32[3,3,384,1536]{2,3,1,0:T(8,128)}), f32[3,3,384,384]{2,3,1,0:T(8,128)}) %reduce-scatter.6.cloned.1.call-update) | async-done | bytes 5308432 | tf_op jit(solution)/shard_map/reduce_scatter | solution.py:35
  1112.3 132.9 %all-gather.8.cloned.1.call-done = f32[1536,3,3,384]{0,3,2,1:T(8,128)} async-done(((f32[384,3,3,384]{0,3,2,1:T(8,128)}), f32[1536,3,3,384]{0,3,2,1:T(8,128)}) %all-gather.8.cloned.1.call-update) | async-done | bytes 21233680 | tf_op jit(solution)/shard_map/all_gather | solution.py:31
  1245.3 150.4 %fusion.68 = f32[5,384,3,3,384,1,1]{1,4,0,3,2,6,5:T(8,128)} fusion(f32[1536,5,384,1,1]{2,0,1,4,3:T(8,128)} %bitcast.293, f32[1536,3,3,384]{0,3,2,1:T(8,128)} %all-gather.8.cloned.1.call-done), kind=kOutput, calls=%fused_computation.46 | convolution fusion | flops 122305904640 | bytes 59572224 | tf_op jit(solution)/shard_map/alc,asub->lcsub/dot_general | solution.py:32
  1395.7 75.5 %fusion.33 = f32[5,3,3,384,384]{3,0,2,1,4:T(8,128)} fusion(f32[5,384,3,3,384,1,1]{1,4,0,3,2,6,5:T(8,128)} %fusion.68, f32[5,5,3,3,3,3]{0,1,3,2,5,4:T(8,128)S(1)} %copy.36), kind=kOutput, calls=%fused_computation.31 | convolution fusion | flops 3583180800 | bytes 53092260 | tf_op jit(solution)/shard_map/lrsutv,lcsub->rtvcb/dot_general | solution.py:33
  1471.2 164.9 %fusion.48 = f32[3,3,384,1536]{2,3,1,0:T(8,128)} fusion(f32[5,3,3,384,384]{3,0,2,1,4:T(8,128)} %fusion.33, f32[384,5,1536]{2,0,1:T(8,128)} %param.6), kind=kOutput, calls=%fused_computation.36 | convolution fusion | flops 122305904640 | bytes 59572224 | tf_op jit(solution)/shard_map/rtvcb,bre->tvce/dot_general | solution.py:34
  1636.2 186.0 %reduce-scatter.8.cloned.1.call-done = f32[3,3,384,384]{2,3,1,0:T(8,128)} async-done(((f32[3,3,384,1536]{2,3,1,0:T(8,128)}), f32[3,3,384,384]{2,3,1,0:T(8,128)}) %reduce-scatter.8.cloned.1.call-update) | async-done | bytes 5308432 | tf_op jit(solution)/shard_map/reduce_scatter | solution.py:35
  1957.3 132.9 %all-gather.10.cloned.1.call-done = f32[1536,3,3,384]{0,3,2,1:T(8,128)} async-done(((f32[384,3,3,384]{0,3,2,1:T(8,128)}), f32[1536,3,3,384]{0,3,2,1:T(8,128)}) %all-gather.10.cloned.1.call-update) | async-done | bytes 21233680 | tf_op jit(solution)/shard_map/all_gather | solution.py:31
  2090.3 150.4 %fusion.71 = f32[5,384,3,3,384,1,1]{1,4,0,3,2,6,5:T(8,128)} fusion(f32[1536,5,384,1,1]{2,0,1,4,3:T(8,128)} %bitcast.294, f32[1536,3,3,384]{0,3,2,1:T(8,128)} %all-gather.10.cloned.1.call-done), kind=kOutput, calls=%fused_computation.47 | convolution fusion | flops 122305904640 | bytes 59572224 | tf_op jit(solution)/shard_map/alc,asub->lcsub/dot_general | solution.py:32
  2240.7 75.5 %fusion.36 = f32[5,3,3,384,384]{3,0,2,1,4:T(8,128)} fusion(f32[5,384,3,3,384,1,1]{1,4,0,3,2,6,5:T(8,128)} %fusion.71, f32[5,5,3,3,3,3]{0,1,3,2,5,4:T(8,128)S(1)} %copy.36), kind=kOutput, calls=%fused_computation.32 | convolution fusion | flops 3583180800 | bytes 53092260 | tf_op jit(solution)/shard_map/lrsutv,lcsub->rtvcb/dot_general | solution.py:33
  2316.3 164.9 %fusion.51 = f32[3,3,384,1536]{2,3,1,0:T(8,128)} fusion(f32[5,3,3,384,384]{3,0,2,1,4:T(8,128)} %fusion.36, f32[384,5,1536]{2,0,1:T(8,128)} %param.6), kind=kOutput, calls=%fused_computation.37 | convolution fusion | flops 122305904640 | bytes 59572224 | tf_op jit(solution)/shard_map/rtvcb,bre->tvce/dot_general | solution.py:34
  2481.2 186.0 %reduce-scatter.10.cloned.1.call-done = f32[3,3,384,384]{2,3,1,0:T(8,128)} async-done(((f32[3,3,384,1536]{2,3,1,0:T(8,128)}), f32[3,3,384,384]{2,3,1,0:T(8,128)}) %reduce-scatter.10.cloned.1.call-update) | async-done | bytes 5308432 | tf_op jit(solution)/shard_map/reduce_scatter | solution.py:35
  2810.8 132.9 %all-gather.12.cloned.1.call-done = f32[1536,3,3,384]{0,3,2,1:T(8,128)} async-done(((f32[384,3,3,384]{0,3,2,1:T(8,128)}), f32[1536,3,3,384]{0,3,2,1:T(8,128)}) %all-gather.12.cloned.1.call-update) | async-done | bytes 21233680 | tf_op jit(solution)/shard_map/all_gather | solution.py:31
  2943.7 150.4 %fusion.74 = f32[5,384,3,3,384,1,1]{1,4,0,3,2,6,5:T(8,128)} fusion(f32[1536,5,384,1,1]{2,0,1,4,3:T(8,128)} %bitcast.295, f32[1536,3,3,384]{0,3,2,1:T(8,128)} %all-gather.12.cloned.1.call-done), kind=kOutput, calls=%fused_computation.48 | convolution fusion | flops 122305904640 | bytes 59572224 | tf_op jit(solution)/shard_map/alc,asub->lcsub/dot_general | solution.py:32
  3094.2 75.5 %fusion.39 = f32[5,3,3,384,384]{3,0,2,1,4:T(8,128)} fusion(f32[5,384,3,3,384,1,1]{1,4,0,3,2,6,5:T(8,128)} %fusion.74, f32[5,5,3,3,3,3]{0,1,3,2,5,4:T(8,128)S(1)} %copy.36), kind=kOutput, calls=%fused_computation.33 | convolution fusion | flops 3583180800 | bytes 53092260 | tf_op jit(solution)/shard_map/lrsutv,lcsub->rtvcb/dot_general | solution.py:33
  3169.7 164.9 %fusion.54 = f32[3,3,384,1536]{2,3,1,0:T(8,128)} fusion(f32[5,3,3,384,384]{3,0,2,1,4:T(8,128)} %fusion.39, f32[384,5,1536]{2,0,1:T(8,128)} %param.6), kind=kOutput, calls=%fused_computation.38 | convolution fusion | flops 122305904640 | bytes 59572224 | tf_op jit(solution)/shard_map/rtvcb,bre->tvce/dot_general | solution.py:34
  3334.7 186.0 %reduce-scatter.12.cloned.1.call-done = f32[3,3,384,384]{2,3,1,0:T(8,128)} async-done(((f32[3,3,384,1536]{2,3,1,0:T(8,128)}), f32[3,3,384,384]{2,3,1,0:T(8,128)}) %reduce-scatter.12.cloned.1.call-update) | async-done | bytes 5308432 | tf_op jit(solution)/shard_map/reduce_scatter | solution.py:35
  3671.9 132.9 %all-gather.14.cloned.1.call-done = f32[1536,3,3,384]{0,3,2,1:T(8,128)} async-done(((f32[384,3,3,384]{0,3,2,1:T(8,128)}), f32[1536,3,3,384]{0,3,2,1:T(8,128)}) %all-gather.14.cloned.1.call-update) | async-done | bytes 21233680 | tf_op jit(solution)/shard_map/all_gather | solution.py:31
  3804.8 150.4 %fusion.77 = f32[5,384,3,3,384,1,1]{1,4,0,3,2,6,5:T(8,128)} fusion(f32[1536,5,384,1,1]{2,0,1,4,3:T(8,128)} %bitcast.296, f32[1536,3,3,384]{0,3,2,1:T(8,128)} %all-gather.14.cloned.1.call-done), kind=kOutput, calls=%fused_computation.49 | convolution fusion | flops 122305904640 | bytes 59572224 | tf_op jit(solution)/shard_map/alc,asub->lcsub/dot_general | solution.py:32
  3955.3 75.5 %fusion.42 = f32[5,3,3,384,384]{3,0,2,1,4:T(8,128)} fusion(f32[5,384,3,3,384,1,1]{1,4,0,3,2,6,5:T(8,128)} %fusion.77, f32[5,5,3,3,3,3]{0,1,3,2,5,4:T(8,128)S(1)} %copy.36), kind=kOutput, calls=%fused_computation.34 | convolution fusion | flops 3583180800 | bytes 53092260 | tf_op jit(solution)/shard_map/lrsutv,lcsub->rtvcb/dot_general | solution.py:33
  4030.8 164.7 %fusion.57 = f32[3,3,384,1536]{2,3,1,0:T(8,128)} fusion(f32[5,3,3,384,384]{3,0,2,1,4:T(8,128)} %fusion.42, f32[384,5,1536]{2,0,1:T(8,128)} %param.6), kind=kOutput, calls=%fused_computation.39 | convolution fusion | flops 122305904640 | bytes 59572224 | tf_op jit(solution)/shard_map/rtvcb,bre->tvce/dot_general | solution.py:34
  4195.5 186.1 %reduce-scatter.14.cloned.1.call-done = f32[3,3,384,384]{2,3,1,0:T(8,128)} async-done(((f32[3,3,384,1536]{2,3,1,0:T(8,128)}), f32[3,3,384,384]{2,3,1,0:T(8,128)}) %reduce-scatter.14.cloned.1.call-update) | async-done | bytes 5308432 | tf_op jit(solution)/shard_map/reduce_scatter | solution.py:35
  (86 shorter events, 892.0 us)
Async XLA Ops:
  7.2 401.4 %all-gather.6.cloned.1.call-start = ((), (), s32[]{:S(2)}) async-start(), calls=%async_computation.6 | async-start | bytes 26542080 | tf_op jit(solution)/shard_map/all_gather | solution.py:31
  76.0 7.6 copy-start
  76.0 316.9 %all-to-all-start = ((f32[384,5,1536]{0,1,2:T(8,128)}), f32[384,5,1536]{0,1,2:T(8,128)}, u32[]{:S(2)}, u32[]{:S(2)}) async-start(f32[384,5,1536]{0,1,2:T(8,128)} %copy.32), calls=%async_computation | async-start | bytes 37748736 | tf_op jit(solution)/shard_map/all_to_all | solution.py:28
  83.5 902.0 %reduce-scatter.6.cloned.1.call-start = ((), (), s32[]{:S(2)}) async-start(), calls=%async_computation.7 | async-start | bytes 26542080 | tf_op jit(solution)/shard_map/reduce_scatter | solution.py:35
  799.5 445.8 %all-gather.8.cloned.1.call-start = ((), (), s32[]{:S(2)}) async-start(), calls=%async_computation.8 | async-start | bytes 26542080 | tf_op jit(solution)/shard_map/all_gather | solution.py:31
  1112.3 710.0 %reduce-scatter.8.cloned.1.call-start = ((), (), s32[]{:S(2)}) async-start(), calls=%async_computation.9 | async-start | bytes 26542080 | tf_op jit(solution)/shard_map/reduce_scatter | solution.py:35
  1636.2 454.1 %all-gather.10.cloned.1.call-start = ((), (), s32[]{:S(2)}) async-start(), calls=%async_computation.10 | async-start | bytes 26542080 | tf_op jit(solution)/shard_map/all_gather | solution.py:31
  1957.3 710.0 %reduce-scatter.10.cloned.1.call-start = ((), (), s32[]{:S(2)}) async-start(), calls=%async_computation.11 | async-start | bytes 26542080 | tf_op jit(solution)/shard_map/reduce_scatter | solution.py:35
  2481.2 462.5 %all-gather.12.cloned.1.call-start = ((), (), s32[]{:S(2)}) async-start(), calls=%async_computation.12 | async-start | bytes 26542080 | tf_op jit(solution)/shard_map/all_gather | solution.py:31
  2810.7 710.0 %reduce-scatter.12.cloned.1.call-start = ((), (), s32[]{:S(2)}) async-start(), calls=%async_computation.13 | async-start | bytes 26542080 | tf_op jit(solution)/shard_map/reduce_scatter | solution.py:35
  3334.6 470.2 %all-gather.14.cloned.1.call-start = ((), (), s32[]{:S(2)}) async-start(), calls=%async_computation.14 | async-start | bytes 26542080 | tf_op jit(solution)/shard_map/all_gather | solution.py:31
  3671.8 709.8 %reduce-scatter.14.cloned.1.call-start = ((), (), s32[]{:S(2)}) async-start(), calls=%async_computation.15 | async-start | bytes 26542080 | tf_op jit(solution)/shard_map/reduce_scatter | solution.py:35
Sparse Core Ops, SparseCore 0:
  60.0 237.2 all-gather.5
  799.6 185.8 reduce-scatter.5
  1112.4 132.8 all-gather.7
  1636.3 185.8 reduce-scatter.7
  1957.4 132.8 all-gather.9
  2481.3 185.8 reduce-scatter.9
  2810.8 132.8 all-gather.11
  3334.7 185.8 reduce-scatter.11
  3671.9 132.8 all-gather.13
  4195.7 185.8 reduce-scatter.13
where the time goes:
time: 4570 us; the launch traced here: 4560 us
  matrix products  1950 us (43%)
  waiting for transfers between devices  1770 us (39%)
  blocking collectives  520 us (11%)
  other arithmetic  225 us (5%)
  local copies, waits for them, and re-layouts  63.4 us (1%)
    reduce_scatter x5, waiting for transfers between devices, apply_ham(): lax.psum_scatter(part_out, 'right', scatter_dimension=3, tiled=True)  930 us
    dot_general x5, matrix products, apply_ham(): jnp.einsum('rtvcb,bre->tvce', stage_two, env_right, precision=PREC_MODE,...  824 us
    dot_general x5, matrix products, apply_ham(): jnp.einsum('alc,asub->lcsub', left_full, vec_full, precision=PREC_MODE, p...  752 us
    all_gather x5, waiting for transfers between devices, apply_ham(): vec_full = lax.all_gather(in_vec, 'left', axis=0, tiled=True)  532 us
    dot_general x5, matrix products, apply_ham(): jnp.einsum('lrsutv,lcsub->rtvcb', mpo_pair, stage_one, precision=PREC_MOD...  378 us
    psum x10, blocking collectives, global_dots(): return lax.psum(local_dots, BOTH_AXES)  322 us
    all_to_all x1, waiting for transfers between devices, local_fn(): left_full = lax.all_to_all(env_left, 'left', 2, 0, tiled=True)  309 us
    psum x5, blocking collectives, local_fn(): beta_val = jnp.sqrt(lax.psum(jnp.sum(residual * residual), BOTH_AXES))  163 us
  transfers between devices with their start and end apart: 11, of which 10 were waited for; matrix products, arithmetic and copies ran while one was open for 1% of the time, Pallas kernels for 0%

commit v1 on v0

v1 whole, which is shorter than its diff:
```python
import functools
import math
import jax
import jax.numpy as jnp
from jax import lax
from jax.experimental import pallas as pl
from jax.experimental.pallas import tpu as pltpu
from jax.sharding import PartitionSpec as P

KRYLOV_STEPS = 5
N_RIGHT, N_LEFT = 4, 4
N_DEV = N_RIGHT * N_LEFT
MESH = pl.DeviceIdType.MESH
LOC = 384
PHYS = 9
S_CHUNKS = 3
ROWS = 16
KPAD = 368


def ortho_kernel(n_basis, n_chunks, *refs):
    u_in = refs[:n_chunks]
    v_in = refs[n_chunks:n_chunks + 3 * n_basis]
    outs = refs[n_chunks + 3 * n_basis:n_chunks + 3 * n_basis + 3]
    (coef, ubuf, vbuf, xs, rbuf, u_sem, v_sem, o_sem, send_sem, recv_sem) = refs[n_chunks + 3 * n_basis + 3:]
    my_r = lax.axis_index("right")
    my_l = lax.axis_index("left")
    me = my_r * N_LEFT + my_l

    def peer(k):
        p = lax.rem(me + k, N_DEV)
        return (p // N_LEFT, lax.rem(p, N_LEFT))

    rows = LOC // n_chunks
    u_copies = [
        pltpu.make_async_copy(u_in[c], ubuf.at[:, pl.ds(c * rows, rows), :], u_sem.at[c])
        for c in range(n_chunks)
    ]
    v_copies = [
        pltpu.make_async_copy(v_in[3 * i + c], vbuf.at[i, pl.ds(3 * c, 3)], v_sem.at[i, c])
        for i in range(n_basis) for c in range(3)
    ]
    for c in u_copies:
        c.start()
    for c in v_copies:
        c.start()

    barrier = pltpu.get_barrier_semaphore()
    for k in range(1, N_DEV):
        pl.semaphore_signal(barrier, inc=1, device_id=peer(k), device_id_type=MESH)

    step_rows = 16
    per_s = LOC // step_rows
    zero = jnp.zeros((8, LOC), jnp.float32)

    def fold(x):
        return x[:8] + x[8:]

    def loop(body, init):
        def outer(s, carry):
            def inner(b, carry2):
                return body(s, pl.ds(pl.multiple_of(b * step_rows, step_rows), step_rows), carry2)
            return lax.fori_loop(0, per_s, inner, carry)
        return lax.fori_loop(0, PHYS, outer, init)

    def all_sum(phase, accs):
        xs[phase] = jnp.zeros((8, 128), jnp.float32)
        for i, acc in enumerate(accs):
            lanes = acc[:, :128] + acc[:, 128:256] + acc[:, 256:]
            xs[phase, i:i + 1, :] = jnp.sum(lanes, axis=0, keepdims=True)
        rbuf[phase, me] = xs[phase]
        copies = [
            pltpu.make_async_remote_copy(
                src_ref=xs.at[phase],
                dst_ref=rbuf.at[phase, me],
                send_sem=send_sem.at[phase, k - 1],
                recv_sem=recv_sem.at[phase, k - 1],
                device_id=peer(k),
                device_id_type=MESH,
            )
            for k in range(1, N_DEV)
        ]
        for c in copies:
            c.start()
        for c in copies:
            c.wait()
        total = jnp.sum(rbuf[phase], axis=0)
        return [jnp.sum(total[i:i + 1, :], axis=1, keepdims=True) for i in range(len(accs))]

    for c in u_copies:
        c.wait()

    coef[...] = jnp.zeros((8, 128), jnp.float32)
    if n_basis:
        accs = []
        for i in range(n_basis):
            for c in range(3):
                v_copies[3 * i + c].wait()

            def dot_body(s, rng, acc, i=i):
                return acc + fold(ubuf[s, rng, :] * vbuf[i, s, rng, :])

            accs.append(loop(dot_body, zero))
        pl.semaphore_wait(barrier, N_DEV - 1)
        first = all_sum(0, accs)
        coef[0:1, :] = jnp.broadcast_to(first[-1], (1, 128))

        def second_body(s, rng, accs):
            u = ubuf[s, rng, :]
            vs = [vbuf[i, s, rng, :] for i in range(n_basis)]
            for i in range(n_basis):
                u = u - first[i] * vs[i]
            ubuf[s, rng, :] = u
            return tuple(acc + fold(u * v) for acc, v in zip(accs, vs))

        second = all_sum(1, loop(second_body, (zero,) * n_basis))

        def norm_body(s, rng, acc):
            u = ubuf[s, rng, :]
            for i in range(n_basis):
                u = u - second[i] * vbuf[i, s, rng, :]
            ubuf[s, rng, :] = u
            return acc + fold(u * u)

        (square,) = all_sum(2, [loop(norm_body, zero)])
    else:
        acc = loop(lambda s, rng, acc: acc + fold(ubuf[s, rng, :] * ubuf[s, rng, :]), zero)
        pl.semaphore_wait(barrier, N_DEV - 1)
        (square,) = all_sum(2, [acc])
    norm = jnp.sqrt(square)
    coef[1:2, :] = jnp.broadcast_to(norm, (1, 128))
    inv = 1.0 / norm
    out_copies = []
    for c in range(3):
        def scale(s, carry, c=c):
            def inner(b, carry2):
                rng = pl.ds(pl.multiple_of(b * 32, 32), 32)
                ubuf[3 * c + s, rng, :] = ubuf[3 * c + s, rng, :] * inv
                return carry2
            return lax.fori_loop(0, LOC // 32, inner, carry)
        lax.fori_loop(0, 3, scale, 0)
        cp = pltpu.make_async_copy(ubuf.at[pl.ds(3 * c, 3)], outs[c], o_sem.at[c])
        cp.start()
        out_copies.append(cp)
    for cp in out_copies:
        cp.wait()


def orthogonalise(u_chunks, basis, collective_id):
    n_basis, n_chunks = len(basis), len(u_chunks)
    any_spec = pl.BlockSpec(memory_space=pl.ANY)
    flat = [c for v in basis for c in v]
    vec = jax.ShapeDtypeStruct((3, LOC, LOC), jnp.float32)
    phases = 3
    outs = pl.pallas_call(
        functools.partial(ortho_kernel, n_basis, n_chunks),
        out_shape=(vec, vec, vec, jax.ShapeDtypeStruct((8, 128), jnp.float32)),
        in_specs=[any_spec] * (n_chunks + len(flat)),
        out_specs=(any_spec, any_spec, any_spec, pl.BlockSpec(memory_space=pltpu.VMEM)),
        scratch_shapes=[
            pltpu.VMEM((PHYS, LOC, LOC), jnp.float32),
            pltpu.VMEM((max(n_basis, 1), PHYS if n_basis else 1, LOC if n_basis else 8, LOC), jnp.float32),
            pltpu.VMEM((phases, 8, 128), jnp.float32),
            pltpu.VMEM((phases, N_DEV, 8, 128), jnp.float32),
            pltpu.SemaphoreType.DMA((n_chunks,)),
            pltpu.SemaphoreType.DMA((max(n_basis, 1), 3)),
            pltpu.SemaphoreType.DMA((3,)),
            pltpu.SemaphoreType.DMA((phases, N_DEV - 1)),
            pltpu.SemaphoreType.DMA((phases, N_DEV - 1)),
        ],
        compiler_params=pltpu.CompilerParams(
            collective_id=collective_id, has_side_effects=True, vmem_limit_bytes=48 * 2**20),
        cost_estimate=pl.CostEstimate(flops=60_000_000, bytes_accessed=4 * PHYS * LOC * LOC * (n_basis + 2), transcendentals=0),
        name=f"ortho{n_basis}",
    )(*u_chunks, *flat)
    return outs[:3], outs[3]


def split_bf16(x):
    one = x.astype(jnp.bfloat16)
    rest = x - one.astype(jnp.float32)
    two = rest.astype(jnp.bfloat16)
    three = (rest - two.astype(jnp.float32)).astype(jnp.bfloat16)
    return one, two, three


def left_kernel(l_ref, g_ref, o_ref, v_ref):
    depth = N_LEFT * LOC

    @pl.when(pl.program_id(0) == 0)
    def _():
        def body(i, carry):
            rows = pl.multiple_of(i * 64, 64)
            for s in range(3):
                parts = split_bf16(g_ref[s, pl.ds(rows, 64), :])
                for k, part in enumerate(parts):
                    v_ref[pl.ds((2 - k) * depth + rows, 64), s * LOC:(s + 1) * LOC] = part
            return carry
        lax.fori_loop(0, depth // 64, body, 0)

    y = jnp.dot(l_ref[...], v_ref[...], preferred_element_type=jnp.float32)
    y += jnp.dot(l_ref[:, :2 * depth], v_ref[depth:, :], preferred_element_type=jnp.float32)
    y += jnp.dot(l_ref[:, :depth], v_ref[2 * depth:, :], preferred_element_type=jnp.float32)
    for s in range(3):
        o_ref[s, 0] = y[:, s * LOC:(s + 1) * LOC]


def apply_left(left_parts, full):
    depth = N_LEFT * LOC
    return pl.pallas_call(
        left_kernel,
        grid=(5,),
        out_shape=jax.ShapeDtypeStruct((3, 5, LOC, LOC), jnp.float32),
        in_specs=[
            pl.BlockSpec((LOC, 3 * depth), lambda l: (l, 0)),
            pl.BlockSpec((3, depth, LOC), lambda l: (0, 0, 0), pipeline_mode=pl.Buffered(1)),
        ],
        out_specs=pl.BlockSpec((3, 1, LOC, LOC), lambda l: (0, l, 0, 0)),
        scratch_shapes=[pltpu.VMEM((3 * depth, 3 * LOC), jnp.bfloat16)],
        compiler_params=pltpu.CompilerParams(vmem_limit_bytes=56 * 2**20),
        cost_estimate=pl.CostEstimate(
            flops=2 * 6 * 5 * LOC * depth * 3 * LOC, bytes_accessed=35_000_000, transcendentals=0),
        name="left",
    )(left_parts, full)


def right_kernel(n_rows, w_ref, t0, t1, t2, r_hbm, o_ref, x_ref, a_ref, r_ref, r_sem):
    g = pl.program_id(0)
    n_mpo = n_rows // ROWS
    depth = 5 * LOC
    fetch = pltpu.make_async_copy(r_hbm, r_ref, r_sem)

    @pl.when(g == 0)
    def _():
        fetch.start()
        x_ref[...] = jnp.zeros_like(x_ref)

    @pl.when(g < n_mpo)
    def _():
        for half in range(2):
            cols = slice(half * LOC, (half + 1) * LOC)
            for s1, t in enumerate((t0, t1, t2)):
                block = t[:, :, half * 8:(half + 1) * 8, :].reshape(15 * 8, LOC)
                one, two, three = split_bf16(block)
                at = s1 * 120
                for k, part in enumerate((one, two, three, one, two, one)):
                    x_ref[k * KPAD + at:k * KPAD + at + 120, cols] = part
        y = jnp.dot(w_ref[...], x_ref[...], preferred_element_type=jnp.float32)
        row = pl.multiple_of(g * ROWS, ROWS)
        for r in range(5):
            halves = [y[r * 72:(r + 1) * 72, h * LOC:(h + 1) * LOC].reshape(9, 8, LOC) for h in range(2)]
            parts = split_bf16(jnp.concatenate(halves, axis=1))
            for k, part in enumerate(parts):
                at = k * depth + r * LOC
                a_ref[:, pl.ds(row, ROWS), at:at + LOC] = part

    @pl.when(g == n_mpo)
    def _():
        fetch.wait()

    @pl.when(g >= n_mpo)
    def _():
        t1_index = g - n_mpo
        for half in range(2):
            cols = slice(half * 2 * LOC, (half + 1) * 2 * LOC)

            def left(n):
                return a_ref[pl.ds(3 * t1_index, 3), :, :n * depth].reshape(3 * n_rows, n * depth)

            y = jnp.dot(left(3), r_ref[:, cols], preferred_element_type=jnp.float32)
            y += jnp.dot(left(2), r_ref[depth:, cols], preferred_element_type=jnp.float32)
            y += jnp.dot(left(1), r_ref[2 * depth:, cols], preferred_element_type=jnp.float32)
            for d in range(2):
                o_ref[2 * half + d] = y[:, d * LOC:(d + 1) * LOC].reshape(3, n_rows, LOC)


def mpo_weights(mpo_pair):
    mat = jnp.transpose(mpo_pair, (1, 4, 5, 2, 3, 0)).reshape(45, 45)
    kron = (mat[:, None, :, None] * jnp.eye(8, dtype=jnp.float32)[None, :, None, :]).reshape(360, 360)
    one, two, three = [jnp.pad(m, ((0, 0), (0, KPAD - 360))) for m in three_parts(kron)]
    return jnp.concatenate([one, one, one, two, two, three], axis=1)


def apply_right(weights, right_parts, stage_one, first_row, n_rows):
    base = first_row // ROWS
    n_mpo = n_rows // ROWS
    t_spec = pl.BlockSpec((3, 5, ROWS, LOC), lambda g: (0, 0, base + jnp.minimum(g, n_mpo - 1), 0))
    flops = 2 * 360 * 6 * 360 * LOC * (n_rows // 8) + 2 * 6 * PHYS * n_rows * 5 * LOC * N_RIGHT * LOC
    return pl.pallas_call(
        functools.partial(right_kernel, n_rows),
        grid=(n_mpo + 3,),
        out_shape=jax.ShapeDtypeStruct((N_RIGHT, PHYS, n_rows, LOC), jnp.float32),
        in_specs=[
            pl.BlockSpec((360, 6 * KPAD), lambda g: (0, 0)), t_spec, t_spec, t_spec,
            pl.BlockSpec(memory_space=pl.ANY),
        ],
        out_specs=pl.BlockSpec((N_RIGHT, 3, n_rows, LOC), lambda g: (0, jnp.maximum(g - n_mpo, 0), 0, 0)),
        scratch_shapes=[
            pltpu.VMEM((6 * KPAD, 2 * LOC), jnp.bfloat16),
            pltpu.VMEM((PHYS, n_rows, 15 * LOC), jnp.bfloat16),
            pltpu.VMEM((15 * LOC, N_RIGHT * LOC), jnp.bfloat16),
            pltpu.SemaphoreType.DMA,
        ],
        compiler_params=pltpu.CompilerParams(vmem_limit_bytes=60 * 2**20),
        cost_estimate=pl.CostEstimate(flops=flops, bytes_accessed=40_000_000, transcendentals=0),
        name="right",
    )(weights, *stage_one, right_parts)


def three_parts(mat):
    one = lax.reduce_precision(mat, 8, 7)
    two = lax.reduce_precision(mat - one, 8, 7)
    three = lax.reduce_precision(mat - one - two, 8, 7)
    return [m.astype(jnp.bfloat16) for m in (one, two, three)]


def solution(mesh):
    psi_spec = P("left", None, None, "right")
    row_chunks = ((0, 128), (128, 128), (256, 128))

    def local_fn(psi_loc, env_left, env_right, mpo_pair):
        left_mat = jnp.transpose(env_left, (1, 0, 2)).reshape(5 * LOC, N_LEFT * LOC)
        right_mat = jnp.transpose(env_right, (1, 0, 2)).reshape(5 * LOC, N_RIGHT * LOC)
        weights = mpo_weights(mpo_pair)
        left_parts = jnp.concatenate(three_parts(left_mat), axis=1)
        right_parts = jnp.concatenate(three_parts(right_mat)[::-1], axis=0)
        psi = jnp.transpose(psi_loc.reshape(LOC, PHYS, LOC), (1, 0, 2))

        def apply_ham(chunks):
            stage_one = []
            for c in chunks:
                full = lax.all_gather(c, "left", axis=1, tiled=True)
                stage_one.append(apply_left(left_parts, full))
            out = []
            for first_row, n_rows in row_chunks:
                part = apply_right(weights, right_parts, stage_one, first_row, n_rows)
                part = lax.psum_scatter(part, "right", scatter_dimension=0, tiled=True)
                out.append(part.reshape(PHYS, n_rows, LOC))
            return out

        vec, _ = orthogonalise([psi], [], 0)
        basis = [vec]
        alpha_list, beta_list = [], []
        for step in range(KRYLOV_STEPS):
            residual = apply_ham(basis[-1])
            vec, coef = orthogonalise(residual, basis, step + 1)
            alpha_list.append(coef[0, 0])
            beta_list.append(coef[1, 0])
            basis.append(vec)
        out_scale = math.sqrt(float(PHYS * LOC * LOC * N_DEV))
        last = jnp.concatenate(basis[-1], axis=0) * out_scale
        psi_next = jnp.transpose(last, (1, 0, 2)).reshape(LOC, 3, 3, LOC)
        return jnp.stack(alpha_list), jnp.stack(beta_list), psi_next

    return jax.shard_map(
        local_fn,
        mesh=mesh,
        in_specs=(psi_spec, P("left", None, None), P("right", None, None), P()),
        out_specs=(P(), P(), psi_spec),
        check_vma=False,
    )
```

time: 4570 us -> 2770 us (0.61)
  matrix products: 1950 us -> 0 us
  Pallas kernels: 0 us -> 1950 us
  waiting for transfers between devices: 1770 us -> 676 us
  blocking collectives: 520 us -> 0 us
  other arithmetic: 225 us -> 95.9 us
    dot_general x15 -> x0, matrix products: 1950 us -> none  [the longest x5 824 us: apply_ham(): jnp.einsum('rtvcb,bre->tvce', stage_two, env_right, precision=PREC_MODE,...]
    pallas_call x0 -> x36, Pallas kernels: none -> 1950 us  [the longest x15 949 us: apply_right(): pl.pallas_call(functools.partial(right_kernel, n_rows), grid=(n_mpo + 3,)...]
    reduce_scatter x5 -> x0, waiting for transfers between devices: 930 us -> none  [apply_ham(): lax.psum_scatter(part_out, 'right', scatter_dimension=3, tiled=True)]
    psum x16 -> x0, blocking collectives: 520 us -> none  [the longest x10 322 us: global_dots(): return lax.psum(local_dots, BOTH_AXES)]
    unnamed x10 -> x45, waiting for transfers between devices: 0.17 us -> 488 us
    all_gather x5 -> x15, waiting for transfers between devices: 532 us -> 189 us  [apply_ham(): full = lax.all_gather(c, 'left', axis=1, tiled=True)]
    all_to_all x1 -> x0, waiting for transfers between devices: 309 us -> none  [local_fn(): left_full = lax.all_to_all(env_left, 'left', 2, 0, tiled=True)]
    reduce_sum x16 -> x0, other arithmetic: 178 us -> none  [the longest x10 107 us: global_dots(): jnp.sum(basis_vec * residual)]
  transfers between devices with their start and end apart: 11 -> 30, of which waited for: 10 -> 14; matrix products, arithmetic and copies ran while one was open for 1% -> 4% of each run, Pallas kernels for 0% -> 42%
where the time goes in v1:
time: 2770 us; the launch traced here: 2760 us
  Pallas kernels  1950 us (70%)
  waiting for transfers between devices  676 us (24%)
  other arithmetic  95.9 us (3%)
    pallas_call x15, Pallas kernels, apply_right(): pl.pallas_call(functools.partial(right_kernel, n_rows), grid=(n_mpo + 3,)...  949 us
    pallas_call x15, Pallas kernels, apply_left(): pl.pallas_call(left_kernel, grid=(5,), out_shape=jax.ShapeDtypeStruct((3,...  805 us
    unnamed x45, waiting for transfers between devices  488 us
    pallas_call x6, Pallas kernels, orthogonalise(): pl.pallas_call(functools.partial(ortho_kernel, n_basis, n_chunks), out_sh...  197 us
    all_gather x15, waiting for transfers between devices, apply_ham(): full = lax.all_gather(c, 'left', axis=1, tiled=True)  189 us
  transfers between devices with their start and end apart: 30, of which 14 were waited for; matrix products, arithmetic and copies ran while one was open for 4% of the time, Pallas kernels for 42%

profile of v1, /device:TPU:0, one launch (start us, length us, event | category | flops | bytes accessed | tf_op | source)
XLA Modules:
  0.0 2761.0 jit_solution(2089861824195629871)
XLA Ops:
  128.6 54.0 %left.15.t0 = f32[3,5,384,384]{3,2,1,0:T(8,128)} custom-call(bf16[1920,4608]{1,0:T(8,128)(2,1)} %pad_maximum_fusion.l_ref, f32[3,1536,384]{2,1,0:T(8,128)} %all-gather.16.cloned.1.call-done.g_ref), custom_call_target="tpu_custom_call" | custom-call | flops 40768634880 | bytes 35000000 | tf_op jit(solution)/shard_map/left/pallas_call | solution.py:210
  182.5 53.6 %left.16.t1 = f32[3,5,384,384]{3,2,1,0:T(8,128)} custom-call(bf16[1920,4608]{1,0:T(8,128)(2,1)} %pad_maximum_fusion.l_ref, f32[3,1536,384]{2,1,0:T(8,128)} %all-gather.18.cloned.1.call-done.g_ref), custom_call_target="tpu_custom_call" | custom-call | flops 40768634880 | bytes 35000000 | tf_op jit(solution)/shard_map/left/pallas_call | solution.py:210
  289.7 63.1 %right.15 = f32[4,9,128,384]{3,2,1,0:T(8,128)} custom-call(bf16[360,2208]{1,0:T(8,128)(2,1)} %concatenate.12.w_ref, f32[3,5,384,384]{3,2,1,0:T(8,128)} %left.15.t0, f32[3,5,384,384]{3,2,1,0:T(8,128)} %left.16.t1, f32[3,5,384,384]{3,2,1,0:T(8,128)} %left.17.t2, bf16[5760,1536]{1,0:T(8,128)(2,1)} %pad_maximum_fusion.1.r_hbm), custom_call_target="tpu_custom_call" | custom-call | flops 50323783680 | bytes 40000000 | tf_op jit(solution)/shard_map/right/pallas_call | solution.py:289
  352.9 63.2 %right.16 = f32[4,9,128,384]{3,2,1,0:T(8,128)} custom-call(bf16[360,2208]{1,0:T(8,128)(2,1)} %concatenate.12.w_ref, f32[3,5,384,384]{3,2,1,0:T(8,128)} %left.15.t0, f32[3,5,384,384]{3,2,1,0:T(8,128)} %left.16.t1, f32[3,5,384,384]{3,2,1,0:T(8,128)} %left.17.t2, bf16[5760,1536]{1,0:T(8,128)(2,1)} %pad_maximum_fusion.1.r_hbm), custom_call_target="tpu_custom_call" | custom-call | flops 50323783680 | bytes 40000000 | tf_op jit(solution)/shard_map/right/pallas_call | solution.py:289
  416.2 63.5 %right.17 = f32[4,9,128,384]{3,2,1,0:T(8,128)} custom-call(bf16[360,2208]{1,0:T(8,128)(2,1)} %concatenate.12.w_ref, f32[3,5,384,384]{3,2,1,0:T(8,128)} %left.15.t0, f32[3,5,384,384]{3,2,1,0:T(8,128)} %left.16.t1, f32[3,5,384,384]{3,2,1,0:T(8,128)} %left.17.t2, bf16[5760,1536]{1,0:T(8,128)(2,1)} %pad_maximum_fusion.1.r_hbm), custom_call_target="tpu_custom_call" | custom-call | flops 50323783680 | bytes 40000000 | tf_op jit(solution)/shard_map/right/pallas_call | solution.py:289
  499.6 75.5 %reduce-scatter.50.cloned.1.call-done = f32[1,9,128,384]{3,2,1,0:T(8,128)} async-done(((f32[4,9,128,384]{3,2,1,0:T(8,128)}), f32[1,9,128,384]{3,2,1,0:T(8,128)}) %reduce-scatter.50.cloned.1.call-update) | async-done | bytes 1769488
  650.7 53.8 %left.18.t0 = f32[3,5,384,384]{3,2,1,0:T(8,128)} custom-call(bf16[1920,4608]{1,0:T(8,128)(2,1)} %pad_maximum_fusion.l_ref, f32[3,1536,384]{2,1,0:T(8,128)} %all-gather.22.cloned.1.call-done.g_ref), custom_call_target="tpu_custom_call" | custom-call | flops 40768634880 | bytes 35000000 | tf_op jit(solution)/shard_map/left/pallas_call | solution.py:210
  704.5 53.6 %left.19.t1 = f32[3,5,384,384]{3,2,1,0:T(8,128)} custom-call(bf16[1920,4608]{1,0:T(8,128)(2,1)} %pad_maximum_fusion.l_ref, f32[3,1536,384]{2,1,0:T(8,128)} %all-gather.24.cloned.1.call-done.g_ref), custom_call_target="tpu_custom_call" | custom-call | flops 40768634880 | bytes 35000000 | tf_op jit(solution)/shard_map/left/pallas_call | solution.py:210
  811.7 63.3 %right.18 = f32[4,9,128,384]{3,2,1,0:T(8,128)} custom-call(bf16[360,2208]{1,0:T(8,128)(2,1)} %concatenate.12.w_ref, f32[3,5,384,384]{3,2,1,0:T(8,128)} %left.18.t0, f32[3,5,384,384]{3,2,1,0:T(8,128)} %left.19.t1, f32[3,5,384,384]{3,2,1,0:T(8,128)} %left.20.t2, bf16[5760,1536]{1,0:T(8,128)(2,1)} %pad_maximum_fusion.1.r_hbm), custom_call_target="tpu_custom_call" | custom-call | flops 50323783680 | bytes 40000000 | tf_op jit(solution)/shard_map/right/pallas_call | solution.py:289
  875.2 63.1 %right.19 = f32[4,9,128,384]{3,2,1,0:T(8,128)} custom-call(bf16[360,2208]{1,0:T(8,128)(2,1)} %concatenate.12.w_ref, f32[3,5,384,384]{3,2,1,0:T(8,128)} %left.18.t0, f32[3,5,384,384]{3,2,1,0:T(8,128)} %left.19.t1, f32[3,5,384,384]{3,2,1,0:T(8,128)} %left.20.t2, bf16[5760,1536]{1,0:T(8,128)(2,1)} %pad_maximum_fusion.1.r_hbm), custom_call_target="tpu_custom_call" | custom-call | flops 50323783680 | bytes 40000000 | tf_op jit(solution)/shard_map/right/pallas_call | solution.py:289
  938.4 63.4 %right.20 = f32[4,9,128,384]{3,2,1,0:T(8,128)} custom-call(bf16[360,2208]{1,0:T(8,128)(2,1)} %concatenate.12.w_ref, f32[3,5,384,384]{3,2,1,0:T(8,128)} %left.18.t0, f32[3,5,384,384]{3,2,1,0:T(8,128)} %left.19.t1, f32[3,5,384,384]{3,2,1,0:T(8,128)} %left.20.t2, bf16[5760,1536]{1,0:T(8,128)(2,1)} %pad_maximum_fusion.1.r_hbm), custom_call_target="tpu_custom_call" | custom-call | flops 50323783680 | bytes 40000000 | tf_op jit(solution)/shard_map/right/pallas_call | solution.py:289
  1023.5 75.5 %reduce-scatter.56.cloned.1.call-done = f32[1,9,128,384]{3,2,1,0:T(8,128)} async-done(((f32[4,9,128,384]{3,2,1,0:T(8,128)}), f32[1,9,128,384]{3,2,1,0:T(8,128)}) %reduce-scatter.56.cloned.1.call-update) | async-done | bytes 1769488
  1339.7 63.3 %right.21 = f32[4,9,128,384]{3,2,1,0:T(8,128)} custom-call(bf16[360,2208]{1,0:T(8,128)(2,1)} %concatenate.12.w_ref, f32[3,5,384,384]{3,2,1,0:T(8,128)} %left.21.t0, f32[3,5,384,384]{3,2,1,0:T(8,128)} %left.22.t1, f32[3,5,384,384]{3,2,1,0:T(8,128)} %left.23.t2, bf16[5760,1536]{1,0:T(8,128)(2,1)} %pad_maximum_fusion.1.r_hbm), custom_call_target="tpu_custom_call" | custom-call | flops 50323783680 | bytes 40000000 | tf_op jit(solution)/shard_map/right/pallas_call | solution.py:289
  1403.2 63.1 %right.22 = f32[4,9,128,384]{3,2,1,0:T(8,128)} custom-call(bf16[360,2208]{1,0:T(8,128)(2,1)} %concatenate.12.w_ref, f32[3,5,384,384]{3,2,1,0:T(8,128)} %left.21.t0, f32[3,5,384,384]{3,2,1,0:T(8,128)} %left.22.t1, f32[3,5,384,384]{3,2,1,0:T(8,128)} %left.23.t2, bf16[5760,1536]{1,0:T(8,128)(2,1)} %pad_maximum_fusion.1.r_hbm), custom_call_target="tpu_custom_call" | custom-call | flops 50323783680 | bytes 40000000 | tf_op jit(solution)/shard_map/right/pallas_call | solution.py:289
  1466.4 63.4 %right.23 = f32[4,9,128,384]{3,2,1,0:T(8,128)} custom-call(bf16[360,2208]{1,0:T(8,128)(2,1)} %concatenate.12.w_ref, f32[3,5,384,384]{3,2,1,0:T(8,128)} %left.21.t0, f32[3,5,384,384]{3,2,1,0:T(8,128)} %left.22.t1, f32[3,5,384,384]{3,2,1,0:T(8,128)} %left.23.t2, bf16[5760,1536]{1,0:T(8,128)(2,1)} %pad_maximum_fusion.1.r_hbm), custom_call_target="tpu_custom_call" | custom-call | flops 50323783680 | bytes 40000000 | tf_op jit(solution)/shard_map/right/pallas_call | solution.py:289
  1551.4 75.5 %reduce-scatter.62.cloned.1.call-done = f32[1,9,128,384]{3,2,1,0:T(8,128)} async-done(((f32[4,9,128,384]{3,2,1,0:T(8,128)}), f32[1,9,128,384]{3,2,1,0:T(8,128)}) %reduce-scatter.62.cloned.1.call-update) | async-done | bytes 1769488
  1872.5 63.3 %right.24 = f32[4,9,128,384]{3,2,1,0:T(8,128)} custom-call(bf16[360,2208]{1,0:T(8,128)(2,1)} %concatenate.12.w_ref, f32[3,5,384,384]{3,2,1,0:T(8,128)} %left.24.t0, f32[3,5,384,384]{3,2,1,0:T(8,128)} %left.25.t1, f32[3,5,384,384]{3,2,1,0:T(8,128)} %left.26.t2, bf16[5760,1536]{1,0:T(8,128)(2,1)} %pad_maximum_fusion.1.r_hbm), custom_call_target="tpu_custom_call" | custom-call | flops 50323783680 | bytes 40000000 | tf_op jit(solution)/shard_map/right/pallas_call | solution.py:289
  1935.9 63.1 %right.25 = f32[4,9,128,384]{3,2,1,0:T(8,128)} custom-call(bf16[360,2208]{1,0:T(8,128)(2,1)} %concatenate.12.w_ref, f32[3,5,384,384]{3,2,1,0:T(8,128)} %left.24.t0, f32[3,5,384,384]{3,2,1,0:T(8,128)} %left.25.t1, f32[3,5,384,384]{3,2,1,0:T(8,128)} %left.26.t2, bf16[5760,1536]{1,0:T(8,128)(2,1)} %pad_maximum_fusion.1.r_hbm), custom_call_target="tpu_custom_call" | custom-call | flops 50323783680 | bytes 40000000 | tf_op jit(solution)/shard_map/right/pallas_call | solution.py:289
  1999.1 63.4 %right.26 = f32[4,9,128,384]{3,2,1,0:T(8,128)} custom-call(bf16[360,2208]{1,0:T(8,128)(2,1)} %concatenate.12.w_ref, f32[3,5,384,384]{3,2,1,0:T(8,128)} %left.24.t0, f32[3,5,384,384]{3,2,1,0:T(8,128)} %left.25.t1, f32[3,5,384,384]{3,2,1,0:T(8,128)} %left.26.t2, bf16[5760,1536]{1,0:T(8,128)(2,1)} %pad_maximum_fusion.1.r_hbm), custom_call_target="tpu_custom_call" | custom-call | flops 50323783680 | bytes 40000000 | tf_op jit(solution)/shard_map/right/pallas_call | solution.py:289
  2084.3 75.5 %reduce-scatter.68.cloned.1.call-done = f32[1,9,128,384]{3,2,1,0:T(8,128)} async-done(((f32[4,9,128,384]{3,2,1,0:T(8,128)}), f32[1,9,128,384]{3,2,1,0:T(8,128)}) %reduce-scatter.68.cloned.1.call-update) | async-done | bytes 1769488
  2410.3 63.4 %right.27 = f32[4,9,128,384]{3,2,1,0:T(8,128)} custom-call(bf16[360,2208]{1,0:T(8,128)(2,1)} %concatenate.12.w_ref, f32[3,5,384,384]{3,2,1,0:T(8,128)} %left.27.t0, f32[3,5,384,384]{3,2,1,0:T(8,128)} %left.28.t1, f32[3,5,384,384]{3,2,1,0:T(8,128)} %left.29.t2, bf16[5760,1536]{1,0:T(8,128)(2,1)} %pad_maximum_fusion.1.r_hbm), custom_call_target="tpu_custom_call" | custom-call | flops 50323783680 | bytes 40000000 | tf_op jit(solution)/shard_map/right/pallas_call | solution.py:289
  2473.8 63.2 %right.28 = f32[4,9,128,384]{3,2,1,0:T(8,128)} custom-call(bf16[360,2208]{1,0:T(8,128)(2,1)} %concatenate.12.w_ref, f32[3,5,384,384]{3,2,1,0:T(8,128)} %left.27.t0, f32[3,5,384,384]{3,2,1,0:T(8,128)} %left.28.t1, f32[3,5,384,384]{3,2,1,0:T(8,128)} %left.29.t2, bf16[5760,1536]{1,0:T(8,128)(2,1)} %pad_maximum_fusion.1.r_hbm), custom_call_target="tpu_custom_call" | custom-call | flops 50323783680 | bytes 40000000 | tf_op jit(solution)/shard_map/right/pallas_call | solution.py:289
  2537.0 63.2 %right.29 = f32[4,9,128,384]{3,2,1,0:T(8,128)} custom-call(bf16[360,2208]{1,0:T(8,128)(2,1)} %concatenate.12.w_ref, f32[3,5,384,384]{3,2,1,0:T(8,128)} %left.27.t0, f32[3,5,384,384]{3,2,1,0:T(8,128)} %left.28.t1, f32[3,5,384,384]{3,2,1,0:T(8,128)} %left.29.t2, bf16[5760,1536]{1,0:T(8,128)(2,1)} %pad_maximum_fusion.1.r_hbm), custom_call_target="tpu_custom_call" | custom-call | flops 50323783680 | bytes 40000000 | tf_op jit(solution)/shard_map/right/pallas_call | solution.py:289
  2622.1 75.5 %reduce-scatter.74.cloned.1.call-done = f32[1,9,128,384]{3,2,1,0:T(8,128)} async-done(((f32[4,9,128,384]{3,2,1,0:T(8,128)}), f32[1,9,128,384]{3,2,1,0:T(8,128)}) %reduce-scatter.74.cloned.1.call-update) | async-done | bytes 1769488
  (142 shorter events, 1204.0 us)
Async XLA Ops:
  22.8 159.7 %all-gather.18.cloned.1.call-start = ((), (), s32[]{:S(2)}) async-start(), calls=%async_computation.16 | async-start | bytes 8847360 | tf_op jit(solution)/shard_map/all_gather | solution.py:332
  23.6 212.6 %all-gather.20.cloned.1.call-start = ((), (), s32[]{:S(2)}) async-start(), calls=%async_computation.17 | async-start | bytes 8847360 | tf_op jit(solution)/shard_map/all_gather | solution.py:332
  24.3 455.5 %reduce-scatter.46.cloned.1.call-start = ((), (), s32[]{:S(2)}) async-start(), calls=%async_computation.30 | async-start | bytes 8847360
  416.2 158.9 %reduce-scatter.50.cloned.1.call-start = ((), (), s32[]{:S(2)}) async-start(), calls=%async_computation.32 | async-start | bytes 8847360
  479.8 170.9 %all-gather.22.cloned.1.call-start = ((), (), s32[]{:S(2)}) async-start(), calls=%async_computation.18 | async-start | bytes 8847360 | tf_op jit(solution)/shard_map/all_gather | solution.py:332
  602.9 155.2 %all-gather.26.cloned.1.call-start = ((), (), s32[]{:S(2)}) async-start(), calls=%async_computation.20 | async-start | bytes 8847360 | tf_op jit(solution)/shard_map/all_gather | solution.py:332
  603.7 398.3 %reduce-scatter.52.cloned.1.call-start = ((), (), s32[]{:S(2)}) async-start(), calls=%async_computation.33 | async-start | bytes 8847360
  875.1 148.4 %reduce-scatter.54.cloned.1.call-start = ((), (), s32[]{:S(2)}) async-start(), calls=%async_computation.34 | async-start | bytes 8847360
  938.3 160.7 %reduce-scatter.56.cloned.1.call-start = ((), (), s32[]{:S(2)}) async-start(), calls=%async_computation.35 | async-start | bytes 8847360
  1001.9 177.0 %all-gather.28.cloned.1.call-start = ((), (), s32[]{:S(2)}) async-start(), calls=%async_computation.21 | async-start | bytes 8847360 | tf_op jit(solution)/shard_map/all_gather | solution.py:332
  1130.9 155.2 %all-gather.32.cloned.1.call-start = ((), (), s32[]{:S(2)}) async-start(), calls=%async_computation.23 | async-start | bytes 8847360 | tf_op jit(solution)/shard_map/all_gather | solution.py:332
  1131.5 398.4 %reduce-scatter.58.cloned.1.call-start = ((), (), s32[]{:S(2)}) async-start(), calls=%async_computation.36 | async-start | bytes 8847360
  1403.1 148.3 %reduce-scatter.60.cloned.1.call-start = ((), (), s32[]{:S(2)}) async-start(), calls=%async_computation.37 | async-start | bytes 8847360
  1466.3 160.5 %reduce-scatter.62.cloned.1.call-start = ((), (), s32[]{:S(2)}) async-start(), calls=%async_computation.38 | async-start | bytes 8847360
  1529.9 181.7 %all-gather.34.cloned.1.call-start = ((), (), s32[]{:S(2)}) async-start(), calls=%async_computation.24 | async-start | bytes 8847360 | tf_op jit(solution)/shard_map/all_gather | solution.py:332
  1663.7 155.2 %all-gather.38.cloned.1.call-start = ((), (), s32[]{:S(2)}) async-start(), calls=%async_computation.26 | async-start | bytes 8847360 | tf_op jit(solution)/shard_map/all_gather | solution.py:332
  1664.4 398.3 %reduce-scatter.64.cloned.1.call-start = ((), (), s32[]{:S(2)}) async-start(), calls=%async_computation.39 | async-start | bytes 8847360
  1935.9 148.4 %reduce-scatter.66.cloned.1.call-start = ((), (), s32[]{:S(2)}) async-start(), calls=%async_computation.40 | async-start | bytes 8847360
  1999.1 160.7 %reduce-scatter.68.cloned.1.call-start = ((), (), s32[]{:S(2)}) async-start(), calls=%async_computation.41 | async-start | bytes 8847360
  2062.6 186.9 %all-gather.40.cloned.1.call-start = ((), (), s32[]{:S(2)}) async-start(), calls=%async_computation.27 | async-start | bytes 8847360 | tf_op jit(solution)/shard_map/all_gather | solution.py:332
  2201.5 155.2 %all-gather.44.cloned.1.call-start = ((), (), s32[]{:S(2)}) async-start(), calls=%async_computation.29 | async-start | bytes 8847360 | tf_op jit(solution)/shard_map/all_gather | solution.py:332
  2202.1 400.4 %reduce-scatter.70.cloned.1.call-start = ((), (), s32[]{:S(2)}) async-start(), calls=%async_computation.42 | async-start | bytes 8847360
  2473.7 148.4 %reduce-scatter.72.cloned.1.call-start = ((), (), s32[]{:S(2)}) async-start(), calls=%async_computation.43 | async-start | bytes 8847360
  2537.0 160.7 %reduce-scatter.74.cloned.1.call-start = ((), (), s32[]{:S(2)}) async-start(), calls=%async_computation.44 | async-start | bytes 8847360
  (14 other events, 810.4 us)
Sparse Core Ops, SparseCore 0:
  72.0 49.0 all-gather.17
  122.6 49.0 all-gather.19
  353.0 71.0 reduce-scatter.45
  426.9 72.5 reduce-scatter.47
  502.5 72.5 reduce-scatter.49
  652.2 49.0 all-gather.23
  702.9 49.0 all-gather.25
  875.2 72.5 reduce-scatter.51
  950.9 72.5 reduce-scatter.53
  1026.4 72.5 reduce-scatter.55
  1180.3 49.0 all-gather.29
  1230.8 49.0 all-gather.31
  1403.2 72.5 reduce-scatter.57
  1478.7 72.5 reduce-scatter.59
  1554.2 72.5 reduce-scatter.61
  1713.0 49.0 all-gather.35
  1936.0 72.5 reduce-scatter.63
  2011.6 72.5 reduce-scatter.65
  2087.1 72.5 reduce-scatter.67
  2250.9 49.0 all-gather.41
  2301.3 49.0 all-gather.43
  2473.8 72.5 reduce-scatter.69
  2549.5 72.5 reduce-scatter.71
  2625.0 72.5 reduce-scatter.73
  (6 shorter events, 289.7 us)

commit v2 on v1

--- a/solution.py
+++ b/solution.py
@@ -31,11 +31,11 @@
         p = lax.rem(me + k, N_DEV)
         return (p // N_LEFT, lax.rem(p, N_LEFT))
 
-    rows = LOC // n_chunks
-    u_copies = [
-        pltpu.make_async_copy(u_in[c], ubuf.at[:, pl.ds(c * rows, rows), :], u_sem.at[c])
-        for c in range(n_chunks)
-    ]
+    u_copies, first_row = [], 0
+    for c in range(n_chunks):
+        rows = u_in[c].shape[1]
+        u_copies.append(pltpu.make_async_copy(u_in[c], ubuf.at[:, pl.ds(first_row, rows), :], u_sem.at[c]))
+        first_row += rows
     v_copies = [
         pltpu.make_async_copy(v_in[3 * i + c], vbuf.at[i, pl.ds(3 * c, 3)], v_sem.at[i, c])
         for i in range(n_basis) for c in range(3)
@@ -60,7 +60,7 @@
         def outer(s, carry):
             def inner(b, carry2):
                 return body(s, pl.ds(pl.multiple_of(b * step_rows, step_rows), step_rows), carry2)
-            return lax.fori_loop(0, per_s, inner, carry)
+            return lax.fori_loop(0, per_s, inner, carry, unroll=2)
         return lax.fori_loop(0, PHYS, outer, init)
 
     def all_sum(phase, accs):
@@ -137,7 +137,7 @@
                 rng = pl.ds(pl.multiple_of(b * 32, 32), 32)
                 ubuf[3 * c + s, rng, :] = ubuf[3 * c + s, rng, :] * inv
                 return carry2
-            return lax.fori_loop(0, LOC // 32, inner, carry)
+            return lax.fori_loop(0, LOC // 32, inner, carry, unroll=2)
         lax.fori_loop(0, 3, scale, 0)
         cp = pltpu.make_async_copy(ubuf.at[pl.ds(3 * c, 3)], outs[c], o_sem.at[c])
         cp.start()
@@ -184,44 +184,83 @@
     return one, two, three
 
 
-def left_kernel(l_ref, g_ref, o_ref, v_ref):
-    depth = N_LEFT * LOC
+def cut_kernel(along_columns, x_ref, o_ref):
+    width = x_ref.shape[1]
+    for k, part in enumerate(split_bf16(x_ref[...])):
+        if along_columns:
+            o_ref[:, k * width:(k + 1) * width] = part
+        else:
+            o_ref[2 - k] = part
+
+
+def cut(mat, along_columns):
+    rows, width = mat.shape
+    step = 192
+    if along_columns:
+        out, spec = (rows, 3 * width), pl.BlockSpec((step, 3 * width), lambda i: (i, 0))
+    else:
+        out, spec = (3, rows, width), pl.BlockSpec((3, step, width), lambda i: (0, i, 0))
+    parts = pl.pallas_call(
+        functools.partial(cut_kernel, along_columns),
+        grid=(rows // step,),
+        out_shape=jax.ShapeDtypeStruct(out, jnp.bfloat16),
+        in_specs=[pl.BlockSpec((step, width), lambda i: (i, 0))],
+        out_specs=spec,
+        compiler_params=pltpu.CompilerParams(vmem_limit_bytes=32 * 2**20),
+        cost_estimate=pl.CostEstimate(flops=5_000_000_000, bytes_accessed=10 * rows * width, transcendentals=0),
+        name="cut",
+    )(mat)
+    return parts if along_columns else parts.reshape(3 * rows, width)
+
+
+def left_kernel(n_shards, l_ref, g_ref, *refs):
+    o_ref, v_ref = refs[-2:]
+    depth = n_shards * LOC
 
     @pl.when(pl.program_id(0) == 0)
     def _():
-        def body(i, carry):
-            rows = pl.multiple_of(i * 64, 64)
-            for s in range(3):
-                parts = split_bf16(g_ref[s, pl.ds(rows, 64), :])
-                for k, part in enumerate(parts):
-                    v_ref[pl.ds((2 - k) * depth + rows, 64), s * LOC:(s + 1) * LOC] = part
-            return carry
-        lax.fori_loop(0, depth // 64, body, 0)
+        for shard in range(n_shards):
+            source = 0
+            if n_shards > 1:
+                source = lax.rem(lax.axis_index("left") + shard + 1, N_LEFT) * LOC
+
+            def body(i, carry, shard=shard, source=source):
+                rows = pl.multiple_of(i * 64, 64)
+                for s in range(3):
+                    parts = split_bf16(g_ref[s, pl.ds(pl.multiple_of(source + rows, 64), 64), :])
+                    for k, part in enumerate(parts):
+                        v_ref[pl.ds((2 - k) * depth + shard * LOC + rows, 64), s * LOC:(s + 1) * LOC] = part
+                return carry
+            lax.fori_loop(0, LOC // 64, body, 0)
 
     y = jnp.dot(l_ref[...], v_ref[...], preferred_element_type=jnp.float32)
     y += jnp.dot(l_ref[:, :2 * depth], v_ref[depth:, :], preferred_element_type=jnp.float32)
     y += jnp.dot(l_ref[:, :depth], v_ref[2 * depth:, :], preferred_element_type=jnp.float32)
     for s in range(3):
-        o_ref[s, 0] = y[:, s * LOC:(s + 1) * LOC]
-
-
-def apply_left(left_parts, full):
-    depth = N_LEFT * LOC
+        part = y[:, s * LOC:(s + 1) * LOC]
+        o_ref[s, 0] = part if n_shards == 1 else part + refs[0][s, 0]
+
+
+def apply_left(left_parts, vec, partial=None):
+    n_shards = 1 if partial is None else N_LEFT - 1
+    depth = n_shards * LOC
+    t_spec = pl.BlockSpec((3, 1, LOC, LOC), lambda l: (0, l, 0, 0))
+    more = () if partial is None else (partial,)
     return pl.pallas_call(
-        left_kernel,
+        functools.partial(left_kernel, n_shards),
         grid=(5,),
         out_shape=jax.ShapeDtypeStruct((3, 5, LOC, LOC), jnp.float32),
         in_specs=[
             pl.BlockSpec((LOC, 3 * depth), lambda l: (l, 0)),
-            pl.BlockSpec((3, depth, LOC), lambda l: (0, 0, 0), pipeline_mode=pl.Buffered(1)),
-        ],
-        out_specs=pl.BlockSpec((3, 1, LOC, LOC), lambda l: (0, l, 0, 0)),
+            pl.BlockSpec(vec.shape, lambda l: (0, 0, 0), pipeline_mode=pl.Buffered(1)),
+        ] + [t_spec] * len(more),
+        out_specs=t_spec,
         scratch_shapes=[pltpu.VMEM((3 * depth, 3 * LOC), jnp.bfloat16)],
         compiler_params=pltpu.CompilerParams(vmem_limit_bytes=56 * 2**20),
         cost_estimate=pl.CostEstimate(
             flops=2 * 6 * 5 * LOC * depth * 3 * LOC, bytes_accessed=35_000_000, transcendentals=0),
-        name="left",
-    )(left_parts, full)
+        name=f"left{n_shards}",
+    )(left_parts, vec, *more)
 
 
 def right_kernel(n_rows, w_ref, t0, t1, t2, r_hbm, o_ref, x_ref, a_ref, r_ref, r_sem):
@@ -316,21 +355,23 @@
 
 def solution(mesh):
     psi_spec = P("left", None, None, "right")
-    row_chunks = ((0, 128), (128, 128), (256, 128))
+    row_chunks = ((0, 96), (96, 128), (224, 160))
 
     def local_fn(psi_loc, env_left, env_right, mpo_pair):
         left_mat = jnp.transpose(env_left, (1, 0, 2)).reshape(5 * LOC, N_LEFT * LOC)
         right_mat = jnp.transpose(env_right, (1, 0, 2)).reshape(5 * LOC, N_RIGHT * LOC)
         weights = mpo_weights(mpo_pair)
-        left_parts = jnp.concatenate(three_parts(left_mat), axis=1)
-        right_parts = jnp.concatenate(three_parts(right_mat)[::-1], axis=0)
+        me = lax.axis_index("left")
+        shard = lambda k: lax.dynamic_slice(left_mat, (0, lax.rem(me + k, N_LEFT) * LOC), (5 * LOC, LOC))
+        left_own = cut(shard(0), True)
+        left_rest = cut(jnp.concatenate([shard(1), shard(2), shard(3)], axis=1), True)
+        right_parts = cut(right_mat, False)
         psi = jnp.transpose(psi_loc.reshape(LOC, PHYS, LOC), (1, 0, 2))
 
         def apply_ham(chunks):
-            stage_one = []
-            for c in chunks:
-                full = lax.all_gather(c, "left", axis=1, tiled=True)
-                stage_one.append(apply_left(left_parts, full))
+            full = [lax.all_gather(c, "left", axis=1, tiled=True) for c in chunks]
+            own = [apply_left(left_own, c) for c in chunks]
+            stage_one = [apply_left(left_rest, f, t) for f, t in zip(full, own)]
             out = []
             for first_row, n_rows in row_chunks:
                 part = apply_right(weights, right_parts, stage_one, first_row, n_rows)

time: 2770 us -> 2600 us (0.939)
  waiting for transfers between devices: 676 us -> 477 us
  Pallas kernels: 1950 us -> 2040 us
  other arithmetic: 95.9 us -> 12.4 us
    all_gather x15, waiting for transfers between devices: 189 us -> 43.2 us  [apply_ham(): full = [lax.all_gather(c, 'left', axis=1, tiled=True) for c in chunks]]
    pallas_call x15 -> x33, Pallas kernels: 805 us -> 915 us  [the longest x30 904 us: apply_left(): pl.pallas_call(functools.partial(left_kernel, n_shards), grid=(5,), out_s...]
    concatenate x2 -> x1, other arithmetic: 68.3 us -> 3.87 us  [local_fn(): jnp.concatenate([shard(1), shard(2), shard(3)], axis=1)]
    unnamed x45, waiting for transfers between devices: 488 us -> 434 us
  transfers between devices with their start and end apart: 30 -> 30, of which waited for: 14 -> 13; matrix products, arithmetic and copies ran while one was open for 4% -> 1% of each run, Pallas kernels for 42% -> 54%
where the time goes in v2:
time: 2600 us; the launch traced here: 2590 us
  Pallas kernels  2040 us (78%)
  waiting for transfers between devices  477 us (18%)
  local copies, waits for them, and re-layouts  45.8 us (2%)
    pallas_call x15, Pallas kernels, apply_right(): pl.pallas_call(functools.partial(right_kernel, n_rows), grid=(n_mpo + 3,)...  949 us
    pallas_call x30, Pallas kernels, apply_left(): pl.pallas_call(functools.partial(left_kernel, n_shards), grid=(5,), out_s...  904 us
    unnamed x45, waiting for transfers between devices  434 us
    pallas_call x6, Pallas kernels, orthogonalise(): pl.pallas_call(functools.partial(ortho_kernel, n_basis, n_chunks), out_sh...  172 us
  transfers between devices with their start and end apart: 30, of which 13 were waited for; matrix products, arithmetic and copies ran while one was open for 1% of the time, Pallas kernels for 54%

profile of v2, /device:TPU:0, one launch (start us, length us, event | category | flops | bytes accessed | tf_op | source)
XLA Modules:
  0.0 2588.0 jit_solution(12545926468148312690)
XLA Ops:
  209.7 43.5 %left3.17.t2 = f32[3,5,384,384]{3,2,1,0:T(8,128)} custom-call(bf16[1920,3456]{1,0:T(8,128)(2,1)} %copy-done, f32[3,1536,384]{2,1,0:T(8,128)} %all-gather.20.cloned.1.call-done.g_ref, f32[3,5,384,384]{3,2,1,0:T(8,128)} %left1.17.refs_0_), custom_call_target="tpu_custom_call" | custom-call | flops 30576476160 | bytes 35000000 | tf_op jit(solution)/shard_map/left3/pallas_call | solution.py:249
  253.2 48.6 %right.15 = f32[4,9,96,384]{3,2,1,0:T(8,128)} custom-call(bf16[360,2208]{1,0:T(8,128)(2,1)} %concatenate.9.w_ref, f32[3,5,384,384]{3,2,1,0:T(8,128)} %left3.15.t0, f32[3,5,384,384]{3,2,1,0:T(8,128)} %left3.16.t1, f32[3,5,384,384]{3,2,1,0:T(8,128)} %left3.17.t2, bf16[5760,1536]{1,0:T(8,128)(2,1)} %bitcast.48), custom_call_target="tpu_custom_call" | custom-call | flops 37742837760 | bytes 40000000 | tf_op jit(solution)/shard_map/right/pallas_call | solution.py:328
  301.9 63.5 %right.16 = f32[4,9,128,384]{3,2,1,0:T(8,128)} custom-call(bf16[360,2208]{1,0:T(8,128)(2,1)} %concatenate.9.w_ref, f32[3,5,384,384]{3,2,1,0:T(8,128)} %left3.15.t0, f32[3,5,384,384]{3,2,1,0:T(8,128)} %left3.16.t1, f32[3,5,384,384]{3,2,1,0:T(8,128)} %left3.17.t2, bf16[5760,1536]{1,0:T(8,128)(2,1)} %bitcast.49), custom_call_target="tpu_custom_call" | custom-call | flops 50323783680 | bytes 40000000 | tf_op jit(solution)/shard_map/right/pallas_call | solution.py:328
  365.5 77.6 %right.17 = f32[4,9,160,384]{3,2,1,0:T(8,128)} custom-call(bf16[360,2208]{1,0:T(8,128)(2,1)} %concatenate.9.w_ref, f32[3,5,384,384]{3,2,1,0:T(8,128)} %left3.15.t0, f32[3,5,384,384]{3,2,1,0:T(8,128)} %left3.16.t1, f32[3,5,384,384]{3,2,1,0:T(8,128)} %left3.17.t2, bf16[5760,1536]{1,0:T(8,128)(2,1)} %bitcast.50), custom_call_target="tpu_custom_call" | custom-call | flops 62904729600 | bytes 40000000 | tf_op jit(solution)/shard_map/right/pallas_call | solution.py:328
  443.2 84.6 %reduce-scatter.50.cloned.1.call-done = f32[1,9,160,384]{3,2,1,0:T(8,128)} async-done(((f32[4,9,160,384]{3,2,1,0:T(8,128)}), f32[1,9,160,384]{3,2,1,0:T(8,128)}) %reduce-scatter.50.cloned.1.call-update) | async-done | bytes 2211856
  652.1 43.7 %left3.19.t1 = f32[3,5,384,384]{3,2,1,0:T(8,128)} custom-call(bf16[1920,3456]{1,0:T(8,128)(2,1)} %copy-done, f32[3,1536,384]{2,1,0:T(8,128)} %all-gather.24.cloned.1.call-done.g_ref, f32[3,5,384,384]{3,2,1,0:T(8,128)} %left1.19.refs_0_), custom_call_target="tpu_custom_call" | custom-call | flops 30576476160 | bytes 35000000 | tf_op jit(solution)/shard_map/left3/pallas_call | solution.py:249
  746.0 48.8 %right.18 = f32[4,9,96,384]{3,2,1,0:T(8,128)} custom-call(bf16[360,2208]{1,0:T(8,128)(2,1)} %concatenate.9.w_ref, f32[3,5,384,384]{3,2,1,0:T(8,128)} %left3.18.t0, f32[3,5,384,384]{3,2,1,0:T(8,128)} %left3.19.t1, f32[3,5,384,384]{3,2,1,0:T(8,128)} %left3.20.t2, bf16[5760,1536]{1,0:T(8,128)(2,1)} %bitcast.51), custom_call_target="tpu_custom_call" | custom-call | flops 37742837760 | bytes 40000000 | tf_op jit(solution)/shard_map/right/pallas_call | solution.py:328
  794.9 63.2 %right.19 = f32[4,9,128,384]{3,2,1,0:T(8,128)} custom-call(bf16[360,2208]{1,0:T(8,128)(2,1)} %concatenate.9.w_ref, f32[3,5,384,384]{3,2,1,0:T(8,128)} %left3.18.t0, f32[3,5,384,384]{3,2,1,0:T(8,128)} %left3.19.t1, f32[3,5,384,384]{3,2,1,0:T(8,128)} %left3.20.t2, bf16[5760,1536]{1,0:T(8,128)(2,1)} %bitcast.52), custom_call_target="tpu_custom_call" | custom-call | flops 50323783680 | bytes 40000000 | tf_op jit(solution)/shard_map/right/pallas_call | solution.py:328
  858.2 77.8 %right.20 = f32[4,9,160,384]{3,2,1,0:T(8,128)} custom-call(bf16[360,2208]{1,0:T(8,128)(2,1)} %concatenate.9.w_ref, f32[3,5,384,384]{3,2,1,0:T(8,128)} %left3.18.t0, f32[3,5,384,384]{3,2,1,0:T(8,128)} %left3.19.t1, f32[3,5,384,384]{3,2,1,0:T(8,128)} %left3.20.t2, bf16[5760,1536]{1,0:T(8,128)(2,1)} %bitcast.53), custom_call_target="tpu_custom_call" | custom-call | flops 62904729600 | bytes 40000000 | tf_op jit(solution)/shard_map/right/pallas_call | solution.py:328
  936.1 86.2 %reduce-scatter.56.cloned.1.call-done = f32[1,9,160,384]{3,2,1,0:T(8,128)} async-done(((f32[4,9,160,384]{3,2,1,0:T(8,128)}), f32[1,9,160,384]{3,2,1,0:T(8,128)}) %reduce-scatter.56.cloned.1.call-update) | async-done | bytes 2211856
  1150.1 43.5 %left3.22.t1 = f32[3,5,384,384]{3,2,1,0:T(8,128)} custom-call(bf16[1920,3456]{1,0:T(8,128)(2,1)} %copy-done, f32[3,1536,384]{2,1,0:T(8,128)} %all-gather.30.cloned.1.call-done.g_ref, f32[3,5,384,384]{3,2,1,0:T(8,128)} %left1.22.refs_0_), custom_call_target="tpu_custom_call" | custom-call | flops 30576476160 | bytes 35000000 | tf_op jit(solution)/shard_map/left3/pallas_call | solution.py:249
  1243.8 49.0 %right.21 = f32[4,9,96,384]{3,2,1,0:T(8,128)} custom-call(bf16[360,2208]{1,0:T(8,128)(2,1)} %concatenate.9.w_ref, f32[3,5,384,384]{3,2,1,0:T(8,128)} %left3.21.t0, f32[3,5,384,384]{3,2,1,0:T(8,128)} %left3.22.t1, f32[3,5,384,384]{3,2,1,0:T(8,128)} %left3.23.t2, bf16[5760,1536]{1,0:T(8,128)(2,1)} %bitcast.54), custom_call_target="tpu_custom_call" | custom-call | flops 37742837760 | bytes 40000000 | tf_op jit(solution)/shard_map/right/pallas_call | solution.py:328
  1292.9 63.2 %right.22 = f32[4,9,128,384]{3,2,1,0:T(8,128)} custom-call(bf16[360,2208]{1,0:T(8,128)(2,1)} %concatenate.9.w_ref, f32[3,5,384,384]{3,2,1,0:T(8,128)} %left3.21.t0, f32[3,5,384,384]{3,2,1,0:T(8,128)} %left3.22.t1, f32[3,5,384,384]{3,2,1,0:T(8,128)} %left3.23.t2, bf16[5760,1536]{1,0:T(8,128)(2,1)} %bitcast.55), custom_call_target="tpu_custom_call" | custom-call | flops 50323783680 | bytes 40000000 | tf_op jit(solution)/shard_map/right/pallas_call | solution.py:328
  1356.2 77.8 %right.23 = f32[4,9,160,384]{3,2,1,0:T(8,128)} custom-call(bf16[360,2208]{1,0:T(8,128)(2,1)} %concatenate.9.w_ref, f32[3,5,384,384]{3,2,1,0:T(8,128)} %left3.21.t0, f32[3,5,384,384]{3,2,1,0:T(8,128)} %left3.22.t1, f32[3,5,384,384]{3,2,1,0:T(8,128)} %left3.23.t2, bf16[5760,1536]{1,0:T(8,128)(2,1)} %bitcast.56), custom_call_target="tpu_custom_call" | custom-call | flops 62904729600 | bytes 40000000 | tf_op jit(solution)/shard_map/right/pallas_call | solution.py:328
  1434.1 86.2 %reduce-scatter.62.cloned.1.call-done = f32[1,9,160,384]{3,2,1,0:T(8,128)} async-done(((f32[4,9,160,384]{3,2,1,0:T(8,128)}), f32[1,9,160,384]{3,2,1,0:T(8,128)}) %reduce-scatter.62.cloned.1.call-update) | async-done | bytes 2211856
  1745.9 48.8 %right.24 = f32[4,9,96,384]{3,2,1,0:T(8,128)} custom-call(bf16[360,2208]{1,0:T(8,128)(2,1)} %concatenate.9.w_ref, f32[3,5,384,384]{3,2,1,0:T(8,128)} %left3.24.t0, f32[3,5,384,384]{3,2,1,0:T(8,128)} %left3.25.t1, f32[3,5,384,384]{3,2,1,0:T(8,128)} %left3.26.t2, bf16[5760,1536]{1,0:T(8,128)(2,1)} %bitcast.57), custom_call_target="tpu_custom_call" | custom-call | flops 37742837760 | bytes 40000000 | tf_op jit(solution)/shard_map/right/pallas_call | solution.py:328
  1794.9 63.4 %right.25 = f32[4,9,128,384]{3,2,1,0:T(8,128)} custom-call(bf16[360,2208]{1,0:T(8,128)(2,1)} %concatenate.9.w_ref, f32[3,5,384,384]{3,2,1,0:T(8,128)} %left3.24.t0, f32[3,5,384,384]{3,2,1,0:T(8,128)} %left3.25.t1, f32[3,5,384,384]{3,2,1,0:T(8,128)} %left3.26.t2, bf16[5760,1536]{1,0:T(8,128)(2,1)} %bitcast.58), custom_call_target="tpu_custom_call" | custom-call | flops 50323783680 | bytes 40000000 | tf_op jit(solution)/shard_map/right/pallas_call | solution.py:328
  1858.4 77.6 %right.26 = f32[4,9,160,384]{3,2,1,0:T(8,128)} custom-call(bf16[360,2208]{1,0:T(8,128)(2,1)} %concatenate.9.w_ref, f32[3,5,384,384]{3,2,1,0:T(8,128)} %left3.24.t0, f32[3,5,384,384]{3,2,1,0:T(8,128)} %left3.25.t1, f32[3,5,384,384]{3,2,1,0:T(8,128)} %left3.26.t2, bf16[5760,1536]{1,0:T(8,128)(2,1)} %bitcast.59), custom_call_target="tpu_custom_call" | custom-call | flops 62904729600 | bytes 40000000 | tf_op jit(solution)/shard_map/right/pallas_call | solution.py:328
  1936.1 86.2 %reduce-scatter.68.cloned.1.call-done = f32[1,9,160,384]{3,2,1,0:T(8,128)} async-done(((f32[4,9,160,384]{3,2,1,0:T(8,128)}), f32[1,9,160,384]{3,2,1,0:T(8,128)}) %reduce-scatter.68.cloned.1.call-update) | async-done | bytes 2211856
  2157.8 43.7 %left3.28.t1 = f32[3,5,384,384]{3,2,1,0:T(8,128)} custom-call(bf16[1920,3456]{1,0:T(8,128)(2,1)} %copy-done, f32[3,1536,384]{2,1,0:T(8,128)} %all-gather.42.cloned.1.call-done.g_ref, f32[3,5,384,384]{3,2,1,0:T(8,128)} %left1.28.refs_0_), custom_call_target="tpu_custom_call" | custom-call | flops 30576476160 | bytes 35000000 | tf_op jit(solution)/shard_map/left3/pallas_call | solution.py:249
  2251.5 48.8 %right.27 = f32[4,9,96,384]{3,2,1,0:T(8,128)} custom-call(bf16[360,2208]{1,0:T(8,128)(2,1)} %concatenate.9.w_ref, f32[3,5,384,384]{3,2,1,0:T(8,128)} %left3.27.t0, f32[3,5,384,384]{3,2,1,0:T(8,128)} %left3.28.t1, f32[3,5,384,384]{3,2,1,0:T(8,128)} %left3.29.t2, bf16[5760,1536]{1,0:T(8,128)(2,1)} %bitcast.60), custom_call_target="tpu_custom_call" | custom-call | flops 37742837760 | bytes 40000000 | tf_op jit(solution)/shard_map/right/pallas_call | solution.py:328
  2300.4 63.2 %right.28 = f32[4,9,128,384]{3,2,1,0:T(8,128)} custom-call(bf16[360,2208]{1,0:T(8,128)(2,1)} %concatenate.9.w_ref, f32[3,5,384,384]{3,2,1,0:T(8,128)} %left3.27.t0, f32[3,5,384,384]{3,2,1,0:T(8,128)} %left3.28.t1, f32[3,5,384,384]{3,2,1,0:T(8,128)} %left3.29.t2, bf16[5760,1536]{1,0:T(8,128)(2,1)} %bitcast.61), custom_call_target="tpu_custom_call" | custom-call | flops 50323783680 | bytes 40000000 | tf_op jit(solution)/shard_map/right/pallas_call | solution.py:328
  2363.6 77.5 %right.29 = f32[4,9,160,384]{3,2,1,0:T(8,128)} custom-call(bf16[360,2208]{1,0:T(8,128)(2,1)} %concatenate.9.w_ref, f32[3,5,384,384]{3,2,1,0:T(8,128)} %left3.27.t0, f32[3,5,384,384]{3,2,1,0:T(8,128)} %left3.28.t1, f32[3,5,384,384]{3,2,1,0:T(8,128)} %left3.29.t2, bf16[5760,1536]{1,0:T(8,128)(2,1)} %bitcast.62), custom_call_target="tpu_custom_call" | custom-call | flops 62904729600 | bytes 40000000 | tf_op jit(solution)/shard_map/right/pallas_call | solution.py:328
  2443.5 84.0 %reduce-scatter.74.cloned.1.call-done = f32[1,9,160,384]{3,2,1,0:T(8,128)} async-done(((f32[4,9,160,384]{3,2,1,0:T(8,128)}), f32[1,9,160,384]{3,2,1,0:T(8,128)}) %reduce-scatter.74.cloned.1.call-update) | async-done | bytes 2211856
  (165 shorter events, 1022.5 us)
Async XLA Ops:
  22.0 144.4 %all-gather.18.cloned.1.call-start = ((), (), s32[]{:S(2)}) async-start(), calls=%async_computation.16 | async-start | bytes 8847360 | tf_op jit(solution)/shard_map/all_gather | solution.py:372
  22.7 187.0 %all-gather.20.cloned.1.call-start = ((), (), s32[]{:S(2)}) async-start(), calls=%async_computation.17 | async-start | bytes 8847360 | tf_op jit(solution)/shard_map/all_gather | solution.py:372
  23.5 419.6 %reduce-scatter.46.cloned.1.call-start = ((), (), s32[]{:S(2)}) async-start(), calls=%async_computation.30 | async-start | bytes 6635520
  301.9 141.3 %reduce-scatter.48.cloned.1.call-start = ((), (), s32[]{:S(2)}) async-start(), calls=%async_computation.31 | async-start | bytes 8847360
  365.4 162.3 %reduce-scatter.50.cloned.1.call-start = ((), (), s32[]{:S(2)}) async-start(), calls=%async_computation.32 | async-start | bytes 11059200
  443.1 162.1 %all-gather.22.cloned.1.call-start = ((), (), s32[]{:S(2)}) async-start(), calls=%async_computation.18 | async-start | bytes 8847360 | tf_op jit(solution)/shard_map/all_gather | solution.py:372
  553.7 149.0 %all-gather.26.cloned.1.call-start = ((), (), s32[]{:S(2)}) async-start(), calls=%async_computation.20 | async-start | bytes 8847360 | tf_op jit(solution)/shard_map/all_gather | solution.py:372
  554.5 381.6 %reduce-scatter.52.cloned.1.call-start = ((), (), s32[]{:S(2)}) async-start(), calls=%async_computation.33 | async-start | bytes 6635520
  794.9 141.2 %reduce-scatter.54.cloned.1.call-start = ((), (), s32[]{:S(2)}) async-start(), calls=%async_computation.34 | async-start | bytes 8847360
  858.2 164.1 %reduce-scatter.56.cloned.1.call-start = ((), (), s32[]{:S(2)}) async-start(), calls=%async_computation.35 | async-start | bytes 11059200
  936.0 167.0 %all-gather.28.cloned.1.call-start = ((), (), s32[]{:S(2)}) async-start(), calls=%async_computation.21 | async-start | bytes 8847360 | tf_op jit(solution)/shard_map/all_gather | solution.py:372
  1051.7 148.9 %all-gather.32.cloned.1.call-start = ((), (), s32[]{:S(2)}) async-start(), calls=%async_computation.23 | async-start | bytes 8847360 | tf_op jit(solution)/shard_map/all_gather | solution.py:372
  1052.3 381.9 %reduce-scatter.58.cloned.1.call-start = ((), (), s32[]{:S(2)}) async-start(), calls=%async_computation.36 | async-start | bytes 6635520
  1292.9 141.2 %reduce-scatter.60.cloned.1.call-start = ((), (), s32[]{:S(2)}) async-start(), calls=%async_computation.37 | async-start | bytes 8847360
  1356.2 164.2 %reduce-scatter.62.cloned.1.call-start = ((), (), s32[]{:S(2)}) async-start(), calls=%async_computation.38 | async-start | bytes 11059200
  1434.0 171.1 %all-gather.34.cloned.1.call-start = ((), (), s32[]{:S(2)}) async-start(), calls=%async_computation.24 | async-start | bytes 8847360 | tf_op jit(solution)/shard_map/all_gather | solution.py:372
  1553.6 149.0 %all-gather.38.cloned.1.call-start = ((), (), s32[]{:S(2)}) async-start(), calls=%async_computation.26 | async-start | bytes 8847360 | tf_op jit(solution)/shard_map/all_gather | solution.py:372
  1554.4 381.6 %reduce-scatter.64.cloned.1.call-start = ((), (), s32[]{:S(2)}) async-start(), calls=%async_computation.39 | async-start | bytes 6635520
  1858.3 163.9 %reduce-scatter.68.cloned.1.call-start = ((), (), s32[]{:S(2)}) async-start(), calls=%async_computation.41 | async-start | bytes 11059200
  1936.0 174.8 %all-gather.40.cloned.1.call-start = ((), (), s32[]{:S(2)}) async-start(), calls=%async_computation.27 | async-start | bytes 8847360 | tf_op jit(solution)/shard_map/all_gather | solution.py:372
  2059.4 148.9 %all-gather.44.cloned.1.call-start = ((), (), s32[]{:S(2)}) async-start(), calls=%async_computation.29 | async-start | bytes 8847360 | tf_op jit(solution)/shard_map/all_gather | solution.py:372
  2060.0 383.5 %reduce-scatter.70.cloned.1.call-start = ((), (), s32[]{:S(2)}) async-start(), calls=%async_computation.42 | async-start | bytes 6635520
  2300.3 143.2 %reduce-scatter.72.cloned.1.call-start = ((), (), s32[]{:S(2)}) async-start(), calls=%async_computation.43 | async-start | bytes 8847360
  2363.6 163.9 %reduce-scatter.74.cloned.1.call-start = ((), (), s32[]{:S(2)}) async-start(), calls=%async_computation.44 | async-start | bytes 11059200
  (18 other events, 712.2 us)
Sparse Core Ops, SparseCore 0:
  71.2 49.0 all-gather.17
  121.8 49.0 all-gather.19
  302.0 56.3 reduce-scatter.45
  365.5 71.0 reduce-scatter.47
  443.2 84.5 reduce-scatter.49
  603.0 49.0 all-gather.23
  653.7 49.0 all-gather.25
  795.0 57.8 reduce-scatter.51
  858.3 72.5 reduce-scatter.53
  936.1 86.1 reduce-scatter.55
  1101.0 49.0 all-gather.29
  1151.5 49.0 all-gather.31
  1293.0 57.8 reduce-scatter.57
  1356.3 72.5 reduce-scatter.59
  1434.2 86.1 reduce-scatter.61
  1653.6 49.0 all-gather.37
  1794.9 57.8 reduce-scatter.63
  1858.4 72.5 reduce-scatter.65
  1936.1 86.1 reduce-scatter.67
  2108.7 49.0 all-gather.41
  2159.2 49.0 all-gather.43
  2300.4 57.8 reduce-scatter.69
  2363.7 72.5 reduce-scatter.71
  2441.3 86.1 reduce-scatter.73
  (6 shorter events, 289.6 us)
